TPU v7x, 256 devices: a whole 4x4x8 slice. The times are simulated.
256 devices in a mesh: dp: 8 (over x, core), rows: 32 (over y, z).
Axes of the slice: x: 4, y: 4, z: 8, core: 2. Of those that a mesh axis runs over, the one named last changes fastest.
Arguments:
- grads: bfloat16 [2, 4096, 14336], P(None, 'rows', 'dp'), may hold values from -64 to 64
- basis: bfloat16 [2, 4096, 512], P(None, 'rows'), may hold values from -0.09375 to 0.09375
- moment1: float32 [2, 512, 14336], P(None, 'rows', 'dp'), may hold values from -0.3 to 0.3
- moment2: float32 [2, 512, 14336], P(None, 'rows', 'dp'), may hold values from 0.001 to 0.03
- weights: bfloat16 [2, 4096, 14336], P(None, 'rows', 'dp'), may hold values from -0.09375 to 0.09375
Outputs:
- new_weights: bfloat16 [2, 4096, 14336], P(None, 'rows')
- new_moment1: float32 [2, 512, 14336], P(None, 'rows', 'dp')
- new_moment2: float32 [2, 512, 14336], P(None, 'rows', 'dp')
All inputs are finite; a program needn't handle non-finite values.
Results may differ from a plain program's by a relative error of at most 0.00115.
The roundings to bfloat16 on the way count: a program that leaves them out, or rounds other values in their place, can miss the bound.
Values may be sent and summed in bfloat16 or wider, within the bound.
No kernel may reach another device: no remote copies, remote signals or barrier semaphores. Data moves between devices by JAX's collectives and lax.ppermute only.
A program may use at most 64 MiB of HBM per device.

v0:
```python
import math
import jax
import jax.numpy as jnp
from jax import lax
from jax.sharding import Mesh
from jax.sharding import PartitionSpec as P

D = 4096
FF = 14336
MATS = 2
STEP = 10
ROWS = ("rows_0", "rows_1")


def sum_by_axis(x, axes, dim):
    for axis in axes:
        x = lax.psum_scatter(x, axis, scatter_dimension=dim, tiled=True)
    return x


def laid_out(tiles, dim):
    tiles = jnp.moveaxis(tiles, 0, dim)
    shape = tiles.shape
    return tiles.reshape(*shape[:dim], shape[dim] * shape[dim + 1], *shape[dim + 2 :])


def gather_in_order(x, axes, turns):
    tiles = x[None]
    for k in turns:
        tiles = lax.all_gather(tiles, axes[k], axis=0, tiled=True)
    carried = [lax.axis_size(axes[k]) for k in reversed(turns)]
    tiles = tiles.reshape(*carried, *x.shape)
    turned = sorted(range(len(turns)), key=lambda place: turns[len(turns) - 1 - place])
    return tiles.transpose(*turned, *range(len(turns), tiles.ndim)).reshape(-1, *x.shape)


def whole_of(x, axes, turns, dim):
    return laid_out(gather_in_order(x, axes, turns), dim)


def moment_step(projected, moment1, moment2, total):
    limit = 1.0 * math.sqrt(MATS * D * FF)
    scale = limit / jnp.maximum(jnp.sqrt(total), limit)
    scaled = scale * projected
    first = 0.9 * moment1 + 0.1 * scaled
    second = 0.999 * moment2 + 0.001 * scaled * scaled
    first_bias_correction = 1.0 - 0.9**STEP
    second_fix = 1.0 - 0.999**STEP
    low_rank_update = (
        first / first_bias_correction / (jnp.sqrt(second / second_fix) + 1e-08)
    ).astype(jnp.bfloat16)
    return (first, second, low_rank_update)


def local(grads, basis, moment1, moment2, weights):
    grad_wide = grads.astype(jnp.float32)
    own_squares = jnp.sum(grad_wide * grad_wide)
    partial_norm_value = jnp.einsum(
        "yka,ykx->yax", basis, grads, preferred_element_type=jnp.float32
    )
    column_square_sum = jnp.full((lax.axis_size(ROWS),), own_squares, jnp.float32)
    projected, group_squares = (
        sum_by_axis(partial_norm_value, ROWS, 1),
        sum_by_axis(column_square_sum, ROWS, 0),
    )
    total = lax.psum(group_squares[0], "dp")
    first, second, low_rank_update = moment_step(projected, moment1, moment2, total)
    projected_back = jnp.einsum(
        "auw,awl->aul",
        basis,
        whole_of(low_rank_update, ROWS, (0, 1), 1),
        preferred_element_type=jnp.float32,
    )
    fresh = (weights.astype(jnp.float32) - 0.5 * projected_back).astype(jnp.bfloat16)
    whole_rows = lax.all_gather(fresh, "dp", axis=2, tiled=True)
    return (whole_rows, first, second)


def solution(mesh):
    finer = Mesh(mesh.devices.reshape(mesh.shape["dp"], 4, 8), ("dp", "rows_0", "rows_1"))
    in_specs = (
        P(None, ROWS, "dp"),
        P(None, ROWS, None),
        P(None, ROWS, "dp"),
        P(None, ROWS, "dp"),
        P(None, ROWS, "dp"),
    )
    out_specs = (P(None, ROWS, None), P(None, ROWS, "dp"), P(None, ROWS, "dp"))
    return jax.shard_map(local, mesh=finer, in_specs=in_specs, out_specs=out_specs, check_vma=False)
```

profile of v0, /device:TPU:1, one launch (start us, length us, event | category | flops | bytes accessed | tf_op | source)
XLA Modules:
  0.0 268.7 jit_solution(6423044746754964495)
XLA Ops:
  7.2 0.0 reduce-scatter.3.cloned.1.call-start
  7.2 0.9 copy-done
  8.1 5.4 %fusion.5 = f32[2,512,1792]{2,1,0:T(8,128)} fusion(bf16[2,128,512]{2,1,0:T(8,128)(2,1)S(1)} %copy-done, bf16[2,128,1792]{2,1,0:T(8,128)(2,1)} %param.5), kind=kOutput, calls=%fused_computation.9 | convolution fusion | flops 469762048 | bytes 8519680 | tf_op jit(solution)/shard_map/yka,ykx->yax/dot_general | solution.py:58
  13.6 0.0 reduce-scatter.5.cloned.1.call-start
  13.6 78.9 %reduce-scatter.3.cloned.1.call-done = f32[2,128,1792]{2,1,0:T(8,128)} async-done(((f32[2,512,1792]{2,1,0:T(8,128)}), f32[2,128,1792]{2,1,0:T(8,128)}) %reduce-scatter.3.cloned.1.call-update) | async-done | bytes 1835024 | tf_op jit(solution)/shard_map/reduce_scatter | solution.py:17
  92.6 0.0 all-gather.4.cloned.1.call-start
  92.6 0.6 dynamic-slice
  93.9 1.1 multiply_reduce_fusion
  95.0 0.6 broadcast_in_dim.6
  95.6 6.6 %all-reduce = f32[32]{0:T(128)S(1)} all-reduce(f32[32]{0:T(128)S(1)} %broadcast_in_dim.6), channel_id=3, replica_groups=mesh['dp'=8,'rows_0'=4,'rows_1'=8] {'rows_0'}, use_global_device_ids=true, to_apply=%region_1.0.clone | all-reduce | flops 32 | bytes 256
  102.2 0.1 dynamic-slice.1
  102.2 14.4 %all-reduce.1 = f32[8]{0:T(128)S(1)} all-reduce(f32[8]{0:T(128)S(1)} %dynamic-slice.1), channel_id=4, replica_groups=mesh['dp'=8,'rows_0'=4,'rows_1'=8] {'rows_1'}, use_global_device_ids=true, to_apply=%region_2.0.clone | all-reduce | flops 8 | bytes 64
  116.6 0.6 dynamic-slice.2
  117.2 1.2 dynamic-slice.3
  118.5 18.6 %psum.7 = f32[]{:T(128)} all-reduce(f32[]{:T(128)} %bitcast), channel_id=1, replica_groups=mesh['dp'=8,'rows_0'=4,'rows_1'=8] {'dp'}, use_global_device_ids=true, to_apply=%region_3.0 | all-reduce | flops 1 | bytes 8 | tf_op jit(solution)/shard_map/psum | solution.py:66
  137.9 1.8 divide_convert_fusion
  139.7 10.5 %all-gather = bf16[8,16,1792]{2,1,0:T(8,128)(2,1)} all-gather(bf16[2,16,1792]{2,1,0:T(8,128)(2,1)S(1)} %get-tuple-element.12), channel_id=2, replica_groups=mesh['dp'=8,'rows_0'=4,'rows_1'=8] {'rows_0'}, dimensions={0}, use_global_device_ids=true | all-gather | bytes 573440 | tf_op jit(solution)/shard_map/all_gather | solution.py:30
  150.2 0.0 all-gather.6.cloned.1.call-start
  150.3 0.6 copy.17
  150.9 49.1 %all-gather.4.cloned.1.call-done = bf16[32,2,16,1792]{3,2,1,0:T(8,128)(2,1)} async-done(((bf16[4,2,16,1792]{3,2,1,0:T(8,128)(2,1)}), bf16[32,2,16,1792]{3,2,1,0:T(8,128)(2,1)}) %all-gather.4.cloned.1.call-update) | async-done | bytes 3670032 | tf_op jit(solution)/shard_map/all_gather | solution.py:30
  200.0 2.3 copy.19
  202.4 2.5 fusion.2
  204.9 47.1 %all-gather.6.cloned.1.call-done = bf16[2,128,14336]{1,2,0:T(8,128)(2,1)} async-done(((bf16[2,128,1792]{1,2,0:T(8,128)(2,1)}), bf16[2,128,14336]{1,2,0:T(8,128)(2,1)}) %all-gather.6.cloned.1.call-update) | async-done | bytes 7340048 | tf_op jit(solution)/shard_map/all_gather | solution.py:75
  252.0 10.1 %copy.21 = bf16[2,128,14336]{2,1,0:T(8,128)(2,1)} copy(bf16[2,128,14336]{1,2,0:T(8,128)(2,1)} %all-gather.6.cloned.1.call-done) | data formatting | bytes 14680064
  (18 shorter events, 0.1 us)
Async XLA Ops:
  7.2 1.0 copy-start
  7.2 85.4 %reduce-scatter.3.cloned.1.call-start = ((), (), s32[]{:S(2)}) async-start(), calls=%async_computation.2 | async-start | bytes 9175040 | tf_op jit(solution)/shard_map/reduce_scatter | solution.py:17
  13.5 79.1 %copy-start.6 = (u32[256]{0:T(256)S(1)}, u32[256]{0:T(256)}, u32[]{:S(2)}) copy-start(u32[256]{0:T(256)} %constant.26) | copy-start | bytes 3076
  13.5 80.4 %copy-start.1 = (bf16[2,128,1792]{2,1,0:T(8,128)(2,1)S(1)}, bf16[2,128,1792]{2,1,0:T(8,128)(2,1)}, u32[]{:S(2)}) copy-start(bf16[2,128,1792]{2,1,0:T(8,128)(2,1)} %param.5) | copy-start | bytes 2752516
  13.5 103.1 %copy-start.5 = (u32[256]{0:T(256)S(1)}, u32[256]{0:T(256)}, u32[]{:S(2)}) copy-start(u32[256]{0:T(256)} %constant.30) | copy-start | bytes 3076
  13.5 124.3 %copy-start.3 = (f32[2,16,1792]{2,1,0:T(8,128)S(1)}, f32[2,16,1792]{2,1,0:T(8,128)}, u32[]{:S(2)}) copy-start(f32[2,16,1792]{2,1,0:T(8,128)} %param.7) | copy-start | bytes 688132
  13.5 124.4 %copy-start.4 = (f32[2,16,1792]{2,1,0:T(8,128)S(1)}, f32[2,16,1792]{2,1,0:T(8,128)}, u32[]{:S(2)}) copy-start(f32[2,16,1792]{2,1,0:T(8,128)} %param.8) | copy-start | bytes 688132
  13.6 136.7 %copy-start.2 = (bf16[2,128,1792]{2,1,0:T(8,128)(2,1)S(1)}, bf16[2,128,1792]{2,1,0:T(8,128)(2,1)}, u32[]{:S(2)}) copy-start(bf16[2,128,1792]{2,1,0:T(8,128)(2,1)} %param.9) | copy-start | bytes 2752516
  13.6 124.3 %reduce-scatter.5.cloned.1.call-start = ((), (), s32[]{:S(2)}) async-start(), calls=%async_computation.3 | async-start | bytes 2064384 | tf_op jit(solution)/shard_map/reduce_scatter | solution.py:17
  92.6 107.5 %all-gather.4.cloned.1.call-start = ((), (), s32[]{:S(2)}) async-start(), calls=%async_computation.4 | async-start | bytes 4128768 | tf_op jit(solution)/shard_map/all_gather | solution.py:30
  150.2 101.8 %all-gather.6.cloned.1.call-start = ((), (), s32[]{:S(2)}) async-start(), calls=%async_computation.5 | async-start | bytes 8257536 | tf_op jit(solution)/shard_map/all_gather | solution.py:75
Sparse Core Ops, SparseCore 0:
  13.7 78.8 reduce-scatter.2
  95.1 37.1 reduce-scatter.4
  150.4 49.6 all-gather.3
  205.0 46.9 all-gather.5
where the time goes:
time: 269 us
  waiting for transfers between devices  175 us (65%)
  blocking collectives  50.1 us (19%)
  local copies, waits for them, and re-layouts  17.1 us (6%)
  between operations  15.3 us (6%)
  matrix products  7.89 us (3%)
  other arithmetic  2.92 us (1%)
    reduce_scatter x2, waiting for transfers between devices, sum_by_axis(): x = lax.psum_scatter(x, axis, scatter_dimension=dim, tiled=True)  79 us
    all_gather x1, waiting for transfers between devices, gather_in_order(): tiles = lax.all_gather(tiles, axes[k], axis=0, tiled=True)  49.1 us
    all_gather x1, waiting for transfers between devices, local(): whole_rows = lax.all_gather(fresh, 'dp', axis=2, tiled=True)  47.1 us
    unnamed x2, blocking collectives  20.9 us
    psum x1, blocking collectives, local(): total = lax.psum(group_squares[0], 'dp')  18.6 us
    unnamed x20, local copies, waits for them, and re-layouts  14.2 us
    all_gather x1, blocking collectives, gather_in_order(): tiles = lax.all_gather(tiles, axes[k], axis=0, tiled=True)  10.5 us
    dot_general x1, matrix products, local(): jnp.einsum('yka,ykx->yax', basis, grads, preferred_element_type=jnp.float32)  5.38 us
  transfers between devices with their start and end apart: 4, of which 3 were waited for; matrix products, arithmetic and copies ran while one was open for 2% of the time, Pallas kernels for 0%

commit v1 on v0

--- a/solution.py
+++ b/solution.py
@@ -10,6 +10,26 @@
 MATS = 2
 STEP = 10
 ROWS = ("rows_0", "rows_1")
+
+
+def _enter_rails(my_data):
+    n_axis = lax.axis_size("dp")
+    outcome_arr = range(n_axis)
+    runs = list(map(lambda dev_j: (dev_j, (dev_j + 1) % n_axis), range(n_axis)))
+    items = list(map(lambda dev_j: (dev_j, (dev_j - 1) % n_axis), outcome_arr))
+    base_arr, t_next = ([my_data], [my_data])
+    for _ in range(n_axis // 2):
+        base_arr.append(lax.ppermute(base_arr[-1], axis_name="dp", perm=runs))
+    h = 0
+    while h < (n_axis - 1) // 2:
+        main = lax.ppermute(t_next[-1], axis_name="dp", perm=items)
+        t_next.append(main)
+        h = h + 1
+    block_now = jnp.concatenate([*base_arr[::-1], *t_next[1:]], axis=2)
+    found_now = jnp.roll(
+        block_now, shift=(lax.axis_index("dp") - n_axis // 2) * my_data.shape[2], axis=2
+    )
+    return found_now
 
 
 def sum_by_axis(x, axes, dim):
@@ -72,7 +92,7 @@
         preferred_element_type=jnp.float32,
     )
     fresh = (weights.astype(jnp.float32) - 0.5 * projected_back).astype(jnp.bfloat16)
-    whole_rows = lax.all_gather(fresh, "dp", axis=2, tiled=True)
+    whole_rows = _enter_rails(fresh)
     return (whole_rows, first, second)
 
 

time: 269 us -> 292 us (1.086); the launches traced: 269 us -> 286 us
  local copies, waits for them, and re-layouts: 17.1 us -> 31.5 us
  starting transfers between devices: 0.16 us -> 13.7 us
  waiting for transfers between devices: 175 us -> 166 us
    all_gather x1 -> x0, waiting for transfers between devices: 47.1 us -> none  [local(): whole_rows = lax.all_gather(fresh, 'dp', axis=2, tiled=True)]
    ppermute x0 -> x7, waiting for transfers between devices: none -> 37.6 us  [the longest x4 36.7 us: _enter_rails(): base_arr.append(lax.ppermute(base_arr[-1], axis_name='dp', perm=runs))]
    ppermute x0 -> x7, starting transfers between devices: none -> 13.6 us  [the longest x4 9.47 us: _enter_rails(): base_arr.append(lax.ppermute(base_arr[-1], axis_name='dp', perm=runs))]
    unnamed x20 -> x39, local copies, waits for them, and re-layouts: 14.2 us -> 24.4 us
    dynamic_slice x0 -> x1, local copies, waits for them, and re-layouts: none -> 4.04 us  [_enter_rails(): jnp.roll(block_now, shift=(lax.axis_index('dp') - n_axis // 2) * my_data....]
  transfers between devices with their start and end apart: 4 -> 10, of which waited for: 3 -> 8; matrix products, arithmetic and copies ran while one was open for 2% -> 4% of each run, Pallas kernels for 0% -> 0%
where the time goes in v1:
time: 292 us; the launch traced here: 286 us
  waiting for transfers between devices  166 us (57%)
  blocking collectives  50.1 us (17%)
  local copies, waits for them, and re-layouts  31.5 us (11%)
  between operations  15.4 us (5%)
  starting transfers between devices  13.7 us (5%)
  matrix products  6.96 us (2%)
  other arithmetic  2.92 us (1%)
    reduce_scatter x2, waiting for transfers between devices, sum_by_axis(): x = lax.psum_scatter(x, axis, scatter_dimension=dim, tiled=True)  79 us
    all_gather x1, waiting for transfers between devices, gather_in_order(): tiles = lax.all_gather(tiles, axes[k], axis=0, tiled=True)  49.2 us
    ppermute x4, waiting for transfers between devices, _enter_rails(): base_arr.append(lax.ppermute(base_arr[-1], axis_name='dp', perm=runs))  36.7 us
    unnamed x39, local copies, waits for them, and re-layouts  24.4 us
    unnamed x2, blocking collectives  20.9 us
    psum x1, blocking collectives, local(): total = lax.psum(group_squares[0], 'dp')  18.6 us
    all_gather x1, blocking collectives, gather_in_order(): tiles = lax.all_gather(tiles, axes[k], axis=0, tiled=True)  10.5 us
    ppermute x4, starting transfers between devices, _enter_rails(): base_arr.append(lax.ppermute(base_arr[-1], axis_name='dp', perm=runs))  9.47 us
  transfers between devices with their start and end apart: 10, of which 8 were waited for; matrix products, arithmetic and copies ran while one was open for 4% of the time, Pallas kernels for 0%

profile of v1, /device:TPU:1, one launch (start us, length us, event | category | flops | bytes accessed | tf_op | source)
XLA Modules:
  0.0 286.3 jit_solution(5185082146796221445)
XLA Ops:
  8.4 5.4 %fusion.5 = f32[2,512,1792]{2,1,0:T(8,128)} fusion(bf16[2,128,512]{2,1,0:T(8,128)(2,1)S(1)} %copy-done, bf16[2,128,1792]{2,1,0:T(8,128)(2,1)} %param.5), kind=kOutput, calls=%fused_computation.26 | convolution fusion | flops 469762048 | bytes 8519680 | tf_op jit(solution)/shard_map/yka,ykx->yax/dot_general | solution.py:78
  13.9 79.0 %reduce-scatter.3.cloned.1.call-done = f32[2,128,1792]{2,1,0:T(8,128)} async-done(((f32[2,512,1792]{2,1,0:T(8,128)}), f32[2,128,1792]{2,1,0:T(8,128)}) %reduce-scatter.3.cloned.1.call-update) | async-done | bytes 1835024 | tf_op jit(solution)/shard_map/reduce_scatter | solution.py:37
  95.9 6.6 %all-reduce = f32[32]{0:T(128)S(1)} all-reduce(f32[32]{0:T(128)S(1)} %broadcast_in_dim.6), channel_id=3, replica_groups=mesh['dp'=8,'rows_0'=4,'rows_1'=8] {'rows_0'}, use_global_device_ids=true, to_apply=%region_1.0.clone | all-reduce | flops 32 | bytes 256
  102.5 14.4 %all-reduce.1 = f32[8]{0:T(128)S(1)} all-reduce(f32[8]{0:T(128)S(1)} %dynamic-slice.1), channel_id=4, replica_groups=mesh['dp'=8,'rows_0'=4,'rows_1'=8] {'rows_1'}, use_global_device_ids=true, to_apply=%region_2.0.clone | all-reduce | flops 8 | bytes 64
  118.7 18.6 %psum.7 = f32[]{:T(128)} all-reduce(f32[]{:T(128)} %bitcast), channel_id=1, replica_groups=mesh['dp'=8,'rows_0'=4,'rows_1'=8] {'dp'}, use_global_device_ids=true, to_apply=%region_3.0 | all-reduce | flops 1 | bytes 8 | tf_op jit(solution)/shard_map/psum | solution.py:86
  138.1 1.8 divide_convert_fusion
  140.0 10.5 %all-gather = bf16[8,16,1792]{2,1,0:T(8,128)(2,1)} all-gather(bf16[2,16,1792]{2,1,0:T(8,128)(2,1)S(1)} %get-tuple-element.12), channel_id=2, replica_groups=mesh['dp'=8,'rows_0'=4,'rows_1'=8] {'rows_0'}, dimensions={0}, use_global_device_ids=true | all-gather | bytes 573440 | tf_op jit(solution)/shard_map/all_gather | solution.py:50
  151.1 49.2 %all-gather.3.cloned.1.call-done = bf16[32,2,16,1792]{3,2,1,0:T(8,128)(2,1)} async-done(((bf16[4,2,16,1792]{3,2,1,0:T(8,128)(2,1)}), bf16[32,2,16,1792]{3,2,1,0:T(8,128)(2,1)}) %all-gather.3.cloned.1.call-update) | async-done | bytes 3670032 | tf_op jit(solution)/shard_map/all_gather | solution.py:50
  200.3 2.3 copy.19
  202.6 1.6 fusion.2
  204.2 1.9 collective-permute-start
  206.2 10.3 %collective-permute-done = bf16[2,128,1792]{1,2,0:T(8,128)(2,1)S(1)} collective-permute-done((bf16[2,128,1792]{1,2,0:T(8,128)(2,1)S(1)}, bf16[2,128,1792]{1,2,0:T(8,128)(2,1)S(1)}, u32[]{:S(2)}, u32[]{:S(2)}) %collective-permute-start) | collective-permute-done | bytes 917536 | tf_op jit(solution)/shard_map/ppermute | solution.py:22
  216.5 2.5 collective-permute-start.1
  219.1 10.2 %collective-permute-done.1 = bf16[2,128,1792]{1,2,0:T(8,128)(2,1)S(1)} collective-permute-done((bf16[2,128,1792]{1,2,0:T(8,128)(2,1)S(1)}, bf16[2,128,1792]{1,2,0:T(8,128)(2,1)S(1)}, u32[]{:S(2)}, u32[]{:S(2)}) %collective-permute-start.1) | collective-permute-done | bytes 917536 | tf_op jit(solution)/shard_map/ppermute | solution.py:22
  229.3 2.5 collective-permute-start.2
  232.1 2.0 collective-permute-start.5
  234.1 8.1 %collective-permute-done.2 = bf16[2,128,1792]{1,2,0:T(8,128)(2,1)} collective-permute-done((bf16[2,128,1792]{1,2,0:T(8,128)(2,1)S(1)}, bf16[2,128,1792]{1,2,0:T(8,128)(2,1)}, u32[]{:S(2)}, u32[]{:S(2)}) %collective-permute-start.2) | collective-permute-done | bytes 917536 | tf_op jit(solution)/shard_map/ppermute | solution.py:22
  242.1 2.6 collective-permute-start.3
  245.3 2.0 collective-permute-start.6
  247.3 8.1 %collective-permute-done.3 = bf16[2,128,1792]{1,2,0:T(8,128)(2,1)} collective-permute-done((bf16[2,128,1792]{1,2,0:T(8,128)(2,1)}, bf16[2,128,1792]{1,2,0:T(8,128)(2,1)}, u32[]{:S(2)}, u32[]{:S(2)}) %collective-permute-start.3) | collective-permute-done | bytes 917536 | tf_op jit(solution)/shard_map/ppermute | solution.py:22
  256.6 1.3 constant_dynamic-update-slice_fusion.14
  257.9 1.3 constant_dynamic-update-slice_fusion.13
  265.6 4.0 %constant_dynamic-slice_fusion = bf16[2,128,14336]{1,2,0:T(8,128)(2,1)} fusion(bf16[2,128,28672]{1,2,0:T(8,128)(2,1)S(1)} %constant_dynamic-update-slice_fusion, s32[]{:T(128)S(6)} %select_n.14), kind=kLoop, calls=%fused_computation.25 | loop fusion | bytes 14680068 | tf_op jit(solution)/shard_map/jit(_roll_dynamic)/dynamic_slice | solution.py:29
  269.7 10.1 %copy.21 = bf16[2,128,14336]{2,1,0:T(8,128)(2,1)} copy(bf16[2,128,14336]{1,2,0:T(8,128)(2,1)} %constant_dynamic-slice_fusion) | data formatting | bytes 14680064
  (50 shorter events, 14.7 us)
Async XLA Ops:
  7.2 1.2 copy-start
  7.2 85.7 %copy-start.8 = (u32[256]{0:T(256)S(1)}, u32[256]{0:T(256)}, u32[]{:S(2)}) copy-start(u32[256]{0:T(256)} %constant.56) | copy-start | bytes 3076
  7.2 109.7 %copy-start.7 = (u32[256]{0:T(256)S(1)}, u32[256]{0:T(256)}, u32[]{:S(2)}) copy-start(u32[256]{0:T(256)} %constant.60) | copy-start | bytes 3076
  7.2 86.9 %copy-start.1 = (bf16[2,128,1792]{2,1,0:T(8,128)(2,1)S(1)}, bf16[2,128,1792]{2,1,0:T(8,128)(2,1)}, u32[]{:S(2)}) copy-start(bf16[2,128,1792]{2,1,0:T(8,128)(2,1)} %param.5) | copy-start | bytes 2752516
  7.2 130.9 %copy-start.5 = (f32[2,16,1792]{2,1,0:T(8,128)S(1)}, f32[2,16,1792]{2,1,0:T(8,128)}, u32[]{:S(2)}) copy-start(f32[2,16,1792]{2,1,0:T(8,128)} %param.7) | copy-start | bytes 688132
  7.2 130.9 %copy-start.6 = (f32[2,16,1792]{2,1,0:T(8,128)S(1)}, f32[2,16,1792]{2,1,0:T(8,128)}, u32[]{:S(2)}) copy-start(f32[2,16,1792]{2,1,0:T(8,128)} %param.8) | copy-start | bytes 688132
  7.2 143.3 %copy-start.4 = (bf16[2,128,1792]{2,1,0:T(8,128)(2,1)S(1)}, bf16[2,128,1792]{2,1,0:T(8,128)(2,1)}, u32[]{:S(2)}) copy-start(bf16[2,128,1792]{2,1,0:T(8,128)(2,1)} %param.9) | copy-start | bytes 2752516
  7.2 85.6 %reduce-scatter.3.cloned.1.call-start = ((), (), s32[]{:S(2)}) async-start(), calls=%async_computation.2 | async-start | bytes 9175040 | tf_op jit(solution)/shard_map/reduce_scatter | solution.py:37
  13.8 124.3 %reduce-scatter.5.cloned.1.call-start = ((), (), s32[]{:S(2)}) async-start(), calls=%async_computation.3 | async-start | bytes 2064384 | tf_op jit(solution)/shard_map/reduce_scatter | solution.py:37
  92.8 107.5 %all-gather.3.cloned.1.call-start = ((), (), s32[]{:S(2)}) async-start(), calls=%async_computation.4 | async-start | bytes 4128768 | tf_op jit(solution)/shard_map/all_gather | solution.py:50
  204.2 12.3 %collective-permute-start = (bf16[2,128,1792]{1,2,0:T(8,128)(2,1)S(1)}, bf16[2,128,1792]{1,2,0:T(8,128)(2,1)S(1)}, u32[]{:S(2)}, u32[]{:S(2)}) collective-permute-start(bf16[2,128,1792]{1,2,0:T(8,128)(2,1)S(1)} %fusion.2), channel_id=1, source_target_pairs={{0,32},{32,64},{64,96},{96,128},{128,160},{160,192},{192,224},{224... | collective-permute-start | bytes 2752520 | tf_op jit(solution)/shard_map/ppermute | solution.py:22
  216.5 12.8 %collective-permute-start.1 = (bf16[2,128,1792]{1,2,0:T(8,128)(2,1)S(1)}, bf16[2,128,1792]{1,2,0:T(8,128)(2,1)S(1)}, u32[]{:S(2)}, u32[]{:S(2)}) collective-permute-start(bf16[2,128,1792]{1,2,0:T(8,128)(2,1)S(1)} %collective-permute-done), channel_id=1, source_target_pairs={{0,32},{32,64},{64,96},{96,128},{128,160},{160,192},{192,224},{224... | collective-permute-start | bytes 2752520 | tf_op jit(solution)/shard_map/ppermute | solution.py:22
  219.0 13.1 %collective-permute-start.4 = (bf16[2,128,1792]{1,2,0:T(8,128)(2,1)S(1)}, bf16[2,128,1792]{1,2,0:T(8,128)(2,1)S(1)}, u32[]{:S(2)}, u32[]{:S(2)}) collective-permute-start(bf16[2,128,1792]{1,2,0:T(8,128)(2,1)S(1)} %fusion.2), channel_id=1, source_target_pairs={{0,224},{32,0},{64,32},{96,64},{128,96},{160,128},{192,160},{224,1... | collective-permute-start | bytes 2752520 | tf_op jit(solution)/shard_map/ppermute | solution.py:25
  229.3 2.8 copy-start.2
  229.3 12.8 %collective-permute-start.2 = (bf16[2,128,1792]{1,2,0:T(8,128)(2,1)S(1)}, bf16[2,128,1792]{1,2,0:T(8,128)(2,1)}, u32[]{:S(2)}, u32[]{:S(2)}) collective-permute-start(bf16[2,128,1792]{1,2,0:T(8,128)(2,1)S(1)} %collective-permute-done.1), channel_id=1, source_target_pairs={{0,32},{32,64},{64,96},{96,128},{128,160},{160,192},{192,224},{224... | collective-permute-start | bytes 2752520 | tf_op jit(solution)/shard_map/ppermute | solution.py:22
  232.1 13.2 %collective-permute-start.5 = (bf16[2,128,1792]{1,2,0:T(8,128)(2,1)S(1)}, bf16[2,128,1792]{1,2,0:T(8,128)(2,1)}, u32[]{:S(2)}, u32[]{:S(2)}) collective-permute-start(bf16[2,128,1792]{1,2,0:T(8,128)(2,1)S(1)} %collective-permute-done.4), channel_id=1, source_target_pairs={{0,224},{32,0},{64,32},{96,64},{128,96},{160,128},{192,160},{224,1... | collective-permute-start | bytes 2752520 | tf_op jit(solution)/shard_map/ppermute | solution.py:25
  242.1 13.2 %collective-permute-start.3 = (bf16[2,128,1792]{1,2,0:T(8,128)(2,1)}, bf16[2,128,1792]{1,2,0:T(8,128)(2,1)}, u32[]{:S(2)}, u32[]{:S(2)}) collective-permute-start(bf16[2,128,1792]{1,2,0:T(8,128)(2,1)} %collective-permute-done.2), channel_id=1, source_target_pairs={{0,32},{32,64},{64,96},{96,128},{128,160},{160,192},{192,224},{224... | collective-permute-start | bytes 2752520 | tf_op jit(solution)/shard_map/ppermute | solution.py:22
  244.7 18.9 %copy-start.3 = (bf16[2,128,1792]{1,2,0:T(8,128)(2,1)S(1)}, bf16[2,128,1792]{1,2,0:T(8,128)(2,1)}, u32[]{:S(2)}) copy-start(bf16[2,128,1792]{1,2,0:T(8,128)(2,1)} %copy-done.2) | copy-start | bytes 2752516
  245.3 15.6 %collective-permute-start.6 = (bf16[2,128,1792]{1,2,0:T(8,128)(2,1)}, bf16[2,128,1792]{1,2,0:T(8,128)(2,1)S(1)}, u32[]{:S(2)}, u32[]{:S(2)}) collective-permute-start(bf16[2,128,1792]{1,2,0:T(8,128)(2,1)} %collective-permute-done.5), channel_id=1, source_target_pairs={{0,224},{32,0},{64,32},{96,64},{128,96},{160,128},{192,160},{224,1... | collective-permute-start | bytes 2752520 | tf_op jit(solution)/shard_map/ppermute | solution.py:25
Sparse Core Ops, SparseCore 0:
  13.9 78.8 reduce-scatter.2
  95.4 37.1 reduce-scatter.4
  150.6 49.6 all-gather.2
